TPU v7x, 32 devices: a whole 2x2x4 slice. The times are simulated.
32 devices in a mesh: pop: 8 (over y, x, core), row: 4 (over z).
Axes of the slice: x: 2, y: 2, z: 4, core: 2. Of those that a mesh axis runs over, the one named last changes fastest.
Arguments:
- tokens: bfloat16 [384, 16, 4096], P('pop'), may hold values from -6 to 6
- weight: bfloat16 [14336, 4096], P('row', 'pop'), may hold values from -0.09375 to 0.09375
- bank_in: bfloat16 [4096, 128], P('row'), may hold values from -0.09375 to 0.09375
- bank_out: bfloat16 [14336, 128], P('row'), may hold values from -6 to 6
- fitness: int32 [384], P('pop'), may hold values from 0 to 191
- past_seeds: int32 [384, 2, 8], P('pop'), may hold values from 0 to 127
- new_seeds: int32 [384, 2, 8], P('pop'), may hold values from 0 to 127
Outputs:
- hidden: bfloat16 [384, 16, 14336], P('pop', None, 'row')
- new_weight: bfloat16 [14336, 4096], P('row', 'pop')
All inputs are finite; a program needn't handle non-finite values.
Results may differ from a plain program's by a relative error of at most 0.012.
Values may be sent and summed in bfloat16 or wider, within the bound.
No kernel may reach another device: no remote copies, remote signals or barrier semaphores. Data moves between devices by JAX's collectives and lax.ppermute only.
A program may use at most 128 MiB of HBM per device.

v0:
```python
import jax
import jax.numpy as jnp
from jax import lax
from jax.sharding import PartitionSpec as P

NOISE_SCALE = 0.1
STEP_SCALE = 0.03


def one_hots(seeds, width):
    levels = jnp.arange(width, dtype=jnp.int32)
    out_hits = (seeds[:, 0, :, None] == levels).astype(jnp.float32)
    in_hits = (seeds[:, 1, :, None] == levels).astype(jnp.float32)
    return (out_hits, in_hits)


def shards(tokens, weight, bank_in, bank_out, fitness, past_seeds, new_seeds):
    members = fitness.shape[0]
    overall = members * lax.axis_size("pop")
    width = bank_out.shape[1]
    everyone = lax.all_gather(fitness, "pop", axis=0, tiled=True)
    lower_count = jnp.sum((everyone[None, :] < fitness[:, None]).astype(jnp.float32), axis=1)
    equal_count = jnp.sum((everyone[None, :] == fitness[:, None]).astype(jnp.float32), axis=1)
    centered = (lower_count + 0.5 * (equal_count - 1.0)) / (overall - 1.0) - 0.5
    out_hits, in_hits = one_hots(past_seeds, width)
    local_coupling = STEP_SCALE * jnp.einsum("m,mki,mkj->ij", centered, out_hits, in_hits)
    coupling = lax.psum(local_coupling, "pop")
    full_in = lax.all_gather(bank_in, "row", axis=0, tiled=True)
    left_part = jnp.dot(bank_out.astype(jnp.float32), coupling, precision=lax.Precision.HIGHEST)
    features = tokens.shape[2]
    flat_tokens = tokens.reshape(members * tokens.shape[1], features)
    own_offset = lax.axis_index("pop") * weight.shape[1]
    columns = lax.dynamic_slice_in_dim(full_in, own_offset, weight.shape[1], 0).astype(jnp.float32)
    update = jnp.dot(left_part, columns.T, precision=lax.Precision.HIGHEST)
    new_weight = (weight.astype(jnp.float32) + update).astype(jnp.bfloat16)
    columns = flat_tokens
    base_part = lax.dot_general(
        columns,
        lax.all_gather(new_weight, "pop", axis=1, tiled=True),
        (((1,), (1,)), ((), ())),
        preferred_element_type=jnp.float32,
    )
    projected = jnp.dot(flat_tokens, full_in, preferred_element_type=jnp.float32).reshape(
        members, tokens.shape[1], width
    )
    hidden_hits, feature_hits = one_hots(new_seeds, width)
    mixing = jnp.einsum("mkb,mkc->mbc", feature_hits, hidden_hits)
    low_term = (NOISE_SCALE * jnp.einsum("mtb,mbc->mtc", projected, mixing)).astype(jnp.bfloat16)
    extra = lax.dot_general(
        low_term.reshape(flat_tokens.shape[0], width),
        bank_out,
        (((1,), (1,)), ((), ())),
        preferred_element_type=jnp.float32,
    )
    hidden = (
        (base_part + extra).astype(jnp.bfloat16).reshape(members, tokens.shape[1], weight.shape[0])
    )
    return (hidden, new_weight)


def solution(mesh):
    placed = (
        P("pop", None, None),
        P("row", "pop"),
        P("row", None),
        P("row", None),
        P("pop"),
        P("pop", None, None),
        P("pop", None, None),
    )
    return jax.shard_map(
        shards,
        mesh=mesh,
        in_specs=placed,
        out_specs=(P("pop", None, "row"), P("row", "pop")),
        check_vma=False,
    )
```

profile of v0, /device:TPU:0, one launch (start us, length us, event | category | flops | bytes accessed | tf_op | source)
XLA Modules:
  0.0 272.2 jit_solution(11762700354457997980)
XLA Ops:
  8.0 0.0 copy-start
  8.0 0.0 all-reduce.3.cloned.1.call-start
  8.1 1.3 dynamic-slice
  10.0 0.9 dynamic-update-slice
  10.9 9.5 %all-reduce = s32[384]{0:T(512)S(1)} all-reduce(s32[384]{0:T(512)S(1)} %dynamic-update-slice), channel_id=1, replica_groups=mesh['pop'=8,'row'=4] {'pop'}, use_global_device_ids=true, to_apply=%add | all-reduce | flops 384 | bytes 3072
  20.4 0.8 convert_reduce_fusion
  21.2 0.7 slice_bitcast_fusion.3
  21.9 0.1 copy.13
  22.0 0.1 copy.14
  22.1 1.0 fusion.16
  23.1 0.0 all-reduce.3.cloned.1.call-update
  23.2 0.0 all-gather.3.cloned.1.call-start
  23.2 0.5 all-gather.3.cloned.1.call-update
  23.7 0.0 all-gather.5.cloned.1.call-start
  23.8 52.4 %all-reduce.3.cloned.1.call-done = f32[128,128]{1,0:T(8,128)} async-done(((f32[128,128]{1,0:T(8,128)}), f32[128,128]{1,0:T(8,128)}) %all-reduce.3.cloned.1.call-update) | async-done | bytes 65552 | tf_op jit(solution)/shard_map/psum | solution.py:27
  76.2 0.0 copy-done
  76.2 1.8 fusion.31
  77.9 0.0 copy-start.1
  77.9 0.0 all-gather.3.cloned.1.call-done
  78.0 6.2 %add_convert_fusion = bf16[3584,512]{1,0:T(8,128)(2,1)} fusion(bf16[3584,512]{1,0:T(8,128)(2,1)} %param.8, f32[128,3584]{1,0:T(8,128)S(1)} %fusion.31, bf16[4096,128]{1,0:T(8,128)(2,1)} %all-gather.3.cloned.1.call-done, s32[]{:T(128)S(6)} %select_n.3), kind=kOutput, calls=%fused_computation.2 | convolution fusion | flops 2824077312 | bytes 9306116 | tf_op jit(solution)/shard_map/dot_general | solution.py:34
  84.2 0.0 all-gather.5.cloned.1.call-update
  84.2 0.0 copy-done.1
  84.2 0.1 copy.15
  84.3 0.1 copy.16
  84.4 6.3 %fusion.11 = bf16[48,16,128]{2,1,0:T(8,128)(2,1)S(1)} fusion(bf16[48,16,4096]{2,1,0:T(8,128)(2,1)} %param.7, bf16[4096,128]{1,0:T(8,128)(2,1)} %all-gather.3.cloned.1.call-done, s32[48,8]{1,0:T(8,128)S(1)} %copy.16, s32[48,8]{1,0:T(8,128)S(1)} %copy.15), kind=kOutput, calls=%fused_computation.7 | convolution fusion | flops 843350016 | bytes 7539712 | tf_op jit(solution)/shard_map/mtb,mbc->mtc/dot_general | solution.py:48
  90.7 141.8 %all-gather.5.cloned.1.call-done = bf16[3584,4096]{1,0:T(8,128)(2,1)} async-done(((bf16[3584,512]{1,0:T(8,128)(2,1)}), bf16[3584,4096]{1,0:T(8,128)(2,1)}) %all-gather.5.cloned.1.call-update) | async-done | bytes 29360144 | tf_op jit(solution)/shard_map/all_gather | solution.py:39
  232.5 28.2 %fusion.32 = f32[3584,768]{0,1:T(8,128)S(1)} fusion(bf16[3584,4096]{1,0:T(8,128)(2,1)} %all-gather.5.cloned.1.call-done, bf16[768,4096]{1,0:T(8,128)(2,1)} %bitcast.34), kind=kOutput, calls=%fused_computation.33 | convolution fusion | flops 22548578304 | bytes 46661632 | tf_op jit(solution)/shard_map/dot_general | solution.py:37
  260.7 4.0 %fusion = bf16[768,3584]{1,0:T(8,128)(2,1)} fusion(f32[3584,768]{0,1:T(8,128)S(1)} %fusion.32, bf16[768,128]{1,0:T(8,128)(2,1)S(1)} %bitcast.33, bf16[3584,128]{1,0:T(8,128)(2,1)S(1)} %copy-done), kind=kOutput, calls=%fused_computation.1 | convolution fusion | flops 710148096 | bytes 17629184 | tf_op jit(solution)/shard_map/dot_general | solution.py:49
  (3 shorter events, 0.0 us)
Async XLA Ops:
  8.0 68.2 %copy-start = (bf16[3584,128]{1,0:T(8,128)(2,1)S(1)}, bf16[3584,128]{1,0:T(8,128)(2,1)}, u32[]{:S(2)}) copy-start(bf16[3584,128]{1,0:T(8,128)(2,1)} %param.10) | copy-start | bytes 2752516
  8.0 68.1 %all-reduce.3.cloned.1.call-start = ((), (), s32[]{:S(2)}) async-start(), calls=%async_computation | async-start | bytes 131072 | tf_op jit(solution)/shard_map/psum | solution.py:27
  23.2 54.8 %all-gather.3.cloned.1.call-start = ((), (), s32[]{:S(2)}) async-start(), calls=%async_computation.1 | async-start | bytes 1310720 | tf_op jit(solution)/shard_map/all_gather | solution.py:28
  23.7 208.8 %all-gather.5.cloned.1.call-start = ((), (), s32[]{:S(2)}) async-start(), calls=%async_computation.2 | async-start | bytes 33030144 | tf_op jit(solution)/shard_map/all_gather | solution.py:39
  77.9 6.3 %copy-start.1 = (s32[48,2,8]{0,2,1:T(8,128)S(1)}, s32[48,2,8]{0,2,1:T(8,128)}, u32[]{:S(2)}) copy-start(s32[48,2,8]{0,2,1:T(8,128)} %param.13) | copy-start | bytes 9220
Sparse Core Ops, SparseCore 0:
  23.3 52.8 all-reduce.2
  84.3 148.1 all-gather.4
Sparse Core Ops, SparseCore 1:
  25.2 27.5 all-gather.2
where the time goes:
time: 272 us
  waiting for transfers between devices  195 us (72%)
  matrix products  47.6 us (18%)
  between operations  16.2 us (6%)
  blocking collectives  9.49 us (3%)
  local copies, waits for them, and re-layouts  3.23 us (1%)
    all_gather x1, waiting for transfers between devices, shards(): lax.all_gather(new_weight, 'pop', axis=1, tiled=True)  142 us
    psum x1, waiting for transfers between devices, shards(): coupling = lax.psum(local_coupling, 'pop')  52.4 us
    dot_general x1, matrix products, shards(): lax.dot_general(columns, lax.all_gather(new_weight, 'pop', axis=1, tiled=...  28.2 us
    unnamed x1, blocking collectives  9.49 us
    dot_general x1, matrix products, shards(): jnp.einsum('mtb,mbc->mtc', projected, mixing)  6.34 us
    dot_general x1, matrix products, shards(): update = jnp.dot(left_part, columns.T, precision=lax.Precision.HIGHEST)  6.22 us
  transfers between devices with their start and end apart: 3, of which 2 were waited for; matrix products, arithmetic and copies ran while one was open for 3% of the time, Pallas kernels for 0%

commit v1 on v0

--- a/solution.py
+++ b/solution.py
@@ -36,7 +36,7 @@
     columns = flat_tokens
     base_part = lax.dot_general(
         columns,
-        lax.all_gather(new_weight, "pop", axis=1, tiled=True),
+        jnp.concatenate(jax.lax.all_gather(new_weight, axis_name="pop"), axis=1),
         (((1,), (1,)), ((), ())),
         preferred_element_type=jnp.float32,
     )

time: 272 us -> 303 us (1.11)
  local copies, waits for them, and re-layouts: 3.23 us -> 39.2 us
  waiting for transfers between devices: 195 us -> 189 us
    all_gather x0 -> x1, local copies, waits for them, and re-layouts: none -> 36 us  [shards(): jax.lax.all_gather(new_weight, axis_name='pop')]
    all_gather x1, waiting for transfers between devices: 142 us -> 136 us  [shards(): jax.lax.all_gather(new_weight, axis_name='pop')]
where the time goes in v1:
time: 303 us; the launch traced here: 302 us
  waiting for transfers between devices  189 us (62%)
  matrix products  47.3 us (16%)
  local copies, waits for them, and re-layouts  39.2 us (13%)
  between operations  16.2 us (5%)
  blocking collectives  9.49 us (3%)
    all_gather x1, waiting for transfers between devices, shards(): jax.lax.all_gather(new_weight, axis_name='pop')  136 us
    psum x1, waiting for transfers between devices, shards(): coupling = lax.psum(local_coupling, 'pop')  52.4 us
    all_gather x1, local copies, waits for them, and re-layouts, shards(): jax.lax.all_gather(new_weight, axis_name='pop')  36 us
    dot_general x1, matrix products, shards(): lax.dot_general(columns, jnp.concatenate(jax.lax.all_gather(new_weight, a...  28 us
    unnamed x1, blocking collectives  9.49 us
    dot_general x1, matrix products, shards(): jnp.einsum('mtb,mbc->mtc', projected, mixing)  6.34 us
    dot_general x1, matrix products, shards(): update = jnp.dot(left_part, columns.T, precision=lax.Precision.HIGHEST)  6.22 us
  transfers between devices with their start and end apart: 3, of which 2 were waited for; matrix products, arithmetic and copies ran while one was open for 3% of the time, Pallas kernels for 0%

profile of v1, /device:TPU:0, one launch (start us, length us, event | category | flops | bytes accessed | tf_op | source)
XLA Modules:
  0.0 302.2 jit_solution(12458779925300625296)
XLA Ops:
  8.0 0.0 copy-start
  8.0 0.0 all-reduce.3.cloned.1.call-start
  8.1 1.3 dynamic-slice
  10.0 0.9 dynamic-update-slice
  10.9 9.5 %all-reduce = s32[384]{0:T(512)S(1)} all-reduce(s32[384]{0:T(512)S(1)} %dynamic-update-slice), channel_id=1, replica_groups=mesh['pop'=8,'row'=4] {'pop'}, use_global_device_ids=true, to_apply=%add | all-reduce | flops 384 | bytes 3072
  20.4 0.8 convert_reduce_fusion
  21.2 0.7 slice_bitcast_fusion.3
  21.9 0.1 copy.18
  22.0 0.1 copy.19
  22.1 1.0 fusion.16
  23.1 0.0 all-reduce.3.cloned.1.call-update
  23.2 0.0 all-gather.4.cloned.1.call-start
  23.2 0.5 all-gather.4.cloned.1.call-update
  23.7 0.0 all-gather.6.cloned.1.call-start
  23.8 52.4 %all-reduce.3.cloned.1.call-done = f32[128,128]{1,0:T(8,128)} async-done(((f32[128,128]{1,0:T(8,128)}), f32[128,128]{1,0:T(8,128)}) %all-reduce.3.cloned.1.call-update) | async-done | bytes 65552 | tf_op jit(solution)/shard_map/psum | solution.py:27
  76.2 0.0 copy-done
  76.2 1.8 fusion.31
  77.9 0.0 copy-start.1
  77.9 0.0 all-gather.4.cloned.1.call-done
  78.0 6.2 %add_convert_fusion = bf16[3584,512]{1,0:T(8,128)(2,1)} fusion(bf16[3584,512]{1,0:T(8,128)(2,1)} %param.8, f32[128,3584]{1,0:T(8,128)S(1)} %fusion.31, bf16[4096,128]{1,0:T(8,128)(2,1)} %all-gather.4.cloned.1.call-done, s32[]{:T(128)S(6)} %select_n.3), kind=kOutput, calls=%fused_computation.2 | convolution fusion | flops 2824077312 | bytes 9306116 | tf_op jit(solution)/shard_map/dot_general | solution.py:34
  84.2 0.0 all-gather.6.cloned.1.call-update
  84.2 0.0 copy-done.1
  84.2 0.1 copy.21
  84.3 0.1 copy.22
  84.4 6.3 %fusion.11 = bf16[48,16,128]{2,1,0:T(8,128)(2,1)S(1)} fusion(bf16[48,16,4096]{2,1,0:T(8,128)(2,1)} %param.7, bf16[4096,128]{1,0:T(8,128)(2,1)} %all-gather.4.cloned.1.call-done, s32[48,8]{1,0:T(8,128)S(1)} %copy.22, s32[48,8]{1,0:T(8,128)S(1)} %copy.21), kind=kOutput, calls=%fused_computation.7 | convolution fusion | flops 843350016 | bytes 7539712 | tf_op jit(solution)/shard_map/mtb,mbc->mtc/dot_general | solution.py:48
  90.7 136.0 %all-gather.6.cloned.1.call-done = bf16[28672,512]{1,0:T(8,128)(2,1)} async-done(((bf16[3584,512]{1,0:T(8,128)(2,1)}), bf16[28672,512]{1,0:T(8,128)(2,1)}) %all-gather.6.cloned.1.call-update) | async-done | bytes 29360144 | tf_op jit(solution)/shard_map/all_gather | solution.py:39
  226.7 36.0 %copy.20 = bf16[8,3584,512]{1,2,0:T(8,128)(2,1)} copy(bf16[8,3584,512]{2,1,0:T(8,128)(2,1)} %bitcast.36) | data formatting | bytes 58720256 | tf_op jit(solution)/shard_map/all_gather | solution.py:39
  262.7 28.0 %fusion.32 = f32[3584,768]{0,1:T(8,128)S(1)} fusion(bf16[768,4096]{1,0:T(8,128)(2,1)} %bitcast.40, bf16[3584,4096]{0,1:T(8,128)(2,1)} %bitcast.37), kind=kOutput, calls=%fused_computation.33 | convolution fusion | flops 22548578304 | bytes 46661632 | tf_op jit(solution)/shard_map/dot_general | solution.py:37
  290.7 4.0 %fusion = bf16[768,3584]{1,0:T(8,128)(2,1)} fusion(f32[3584,768]{0,1:T(8,128)S(1)} %fusion.32, bf16[768,128]{1,0:T(8,128)(2,1)S(1)} %bitcast.39, bf16[3584,128]{1,0:T(8,128)(2,1)S(1)} %copy-done), kind=kOutput, calls=%fused_computation.1 | convolution fusion | flops 710148096 | bytes 17629184 | tf_op jit(solution)/shard_map/dot_general | solution.py:49
  (3 shorter events, 0.0 us)
Async XLA Ops:
  8.0 68.2 %copy-start = (bf16[3584,128]{1,0:T(8,128)(2,1)S(1)}, bf16[3584,128]{1,0:T(8,128)(2,1)}, u32[]{:S(2)}) copy-start(bf16[3584,128]{1,0:T(8,128)(2,1)} %param.10) | copy-start | bytes 2752516
  8.0 68.1 %all-reduce.3.cloned.1.call-start = ((), (), s32[]{:S(2)}) async-start(), calls=%async_computation | async-start | bytes 131072 | tf_op jit(solution)/shard_map/psum | solution.py:27
  23.2 54.8 %all-gather.4.cloned.1.call-start = ((), (), s32[]{:S(2)}) async-start(), calls=%async_computation.1 | async-start | bytes 1310720 | tf_op jit(solution)/shard_map/all_gather | solution.py:28
  23.7 203.0 %all-gather.6.cloned.1.call-start = ((), (), s32[]{:S(2)}) async-start(), calls=%async_computation.2 | async-start | bytes 33030144 | tf_op jit(solution)/shard_map/all_gather | solution.py:39
  77.9 6.3 %copy-start.1 = (s32[48,2,8]{0,2,1:T(8,128)S(1)}, s32[48,2,8]{0,2,1:T(8,128)}, u32[]{:S(2)}) copy-start(s32[48,2,8]{0,2,1:T(8,128)} %param.13) | copy-start | bytes 9220
Sparse Core Ops, SparseCore 0:
  23.3 52.8 all-reduce.2
  84.3 142.3 all-gather.5
Sparse Core Ops, SparseCore 1:
  25.2 27.5 all-gather.3

commit v2 on v0

--- a/solution.py
+++ b/solution.py
@@ -24,7 +24,11 @@
     centered = (lower_count + 0.5 * (equal_count - 1.0)) / (overall - 1.0) - 0.5
     out_hits, in_hits = one_hots(past_seeds, width)
     local_coupling = STEP_SCALE * jnp.einsum("m,mki,mkj->ij", centered, out_hits, in_hits)
-    coupling = lax.psum(local_coupling, "pop")
+    size = lax.axis_size("pop")
+    coupling, far = (local_coupling, 1)
+    while far < size:
+        coupling = coupling + lax.ppermute(coupling, "pop", [(i, i ^ far) for i in range(size)])
+        far = 2 * far
     full_in = lax.all_gather(bank_in, "row", axis=0, tiled=True)
     left_part = jnp.dot(bank_out.astype(jnp.float32), coupling, precision=lax.Precision.HIGHEST)
     features = tokens.shape[2]

time: 272 us -> 234 us (0.86)
  waiting for transfers between devices: 195 us -> 158 us
    psum x1 -> x0, waiting for transfers between devices: 52.4 us -> none  [shards(): coupling = lax.psum(local_coupling, 'pop')]
    ppermute x0 -> x3, waiting for transfers between devices: none -> 8.39 us  [shards(): lax.ppermute(coupling, 'pop', [(i, i ^ far) for i in range(size)])]
    all_gather x1, waiting for transfers between devices: 0.03 us -> 7.16 us  [shards(): full_in = lax.all_gather(bank_in, 'row', axis=0, tiled=True)]
  transfers between devices with their start and end apart: 3 -> 5, of which waited for: 2 -> 5; matrix products, arithmetic and copies ran while one was open for 3% -> 5% of each run, Pallas kernels for 0% -> 0%
where the time goes in v2:
time: 234 us
  waiting for transfers between devices  158 us (68%)
  matrix products  46.1 us (20%)
  between operations  14.8 us (6%)
  blocking collectives  9.49 us (4%)
  local copies, waits for them, and re-layouts  2.99 us (1%)
    all_gather x1, waiting for transfers between devices, shards(): lax.all_gather(new_weight, 'pop', axis=1, tiled=True)  142 us
    dot_general x1, matrix products, shards(): lax.dot_general(columns, lax.all_gather(new_weight, 'pop', axis=1, tiled=...  28.2 us
    unnamed x1, blocking collectives  9.49 us
    ppermute x3, waiting for transfers between devices, shards(): lax.ppermute(coupling, 'pop', [(i, i ^ far) for i in range(size)])  8.39 us
    all_gather x1, waiting for transfers between devices, shards(): full_in = lax.all_gather(bank_in, 'row', axis=0, tiled=True)  7.16 us
    dot_general x1, matrix products, shards(): jnp.einsum('mtb,mbc->mtc', projected, mixing)  6.34 us
    dot_general x1, matrix products, shards(): update = jnp.dot(left_part, columns.T, precision=lax.Precision.HIGHEST)  6.21 us
  transfers between devices with their start and end apart: 5, of which 5 were waited for; matrix products, arithmetic and copies ran while one was open for 5% of the time, Pallas kernels for 0%

profile of v2, /device:TPU:0, one launch (start us, length us, event | category | flops | bytes accessed | tf_op | source)
XLA Modules:
  0.0 233.9 jit_solution(1218226432475725347)
XLA Ops:
  7.2 0.0 copy-start
  7.2 0.0 all-gather.3.cloned.1.call-start
  7.2 0.7 all-gather.3.cloned.1.call-update
  7.9 0.0 all-gather.5.cloned.1.call-start
  8.0 1.2 dynamic-slice
  9.9 0.9 dynamic-update-slice
  10.7 9.5 %all-reduce = s32[384]{0:T(512)S(1)} all-reduce(s32[384]{0:T(512)S(1)} %dynamic-update-slice), channel_id=1, replica_groups=mesh['pop'=8,'row'=4] {'pop'}, use_global_device_ids=true, to_apply=%add | all-reduce | flops 384 | bytes 3072
  20.2 0.8 convert_reduce_fusion
  21.1 0.7 slice_bitcast_fusion.3
  21.8 0.4 fusion.16
  22.2 0.1 collective-permute-start
  22.3 1.2 collective-permute-done
  23.5 0.9 collective-permute-start.1
  24.4 3.4 %collective-permute-done.1 = f32[128,128]{1,0:T(8,128)S(1)} collective-permute-done((f32[128,128]{1,0:T(8,128)S(1)}, f32[128,128]{1,0:T(8,128)S(1)}, u32[]{:S(2)}, u32[]{:S(2)}) %collective-permute-start.1) | collective-permute-done | bytes 65568 | tf_op jit(solution)/shard_map/ppermute | solution.py:30
  27.9 0.6 collective-permute-start.2
  28.4 3.7 %collective-permute-done.2 = f32[128,128]{1,0:T(8,128)S(1)} collective-permute-done((f32[128,128]{1,0:T(8,128)S(1)}, f32[128,128]{1,0:T(8,128)S(1)}, u32[]{:S(2)}, u32[]{:S(2)}) %collective-permute-start.2) | collective-permute-done | bytes 65568 | tf_op jit(solution)/shard_map/ppermute | solution.py:30
  32.2 0.0 copy-done
  32.2 0.9 fusion.29
  33.1 0.0 copy-start.1
  33.1 7.2 %all-gather.3.cloned.1.call-done = bf16[4096,128]{1,0:T(8,128)(2,1)} async-done(((bf16[1024,128]{1,0:T(8,128)(2,1)}), bf16[4096,128]{1,0:T(8,128)(2,1)}) %all-gather.3.cloned.1.call-update) | async-done | bytes 1048592 | tf_op jit(solution)/shard_map/all_gather | solution.py:32
  40.3 6.2 %add_convert_fusion = bf16[3584,512]{1,0:T(8,128)(2,1)} fusion(bf16[3584,512]{1,0:T(8,128)(2,1)} %param.8, f32[128,3584]{1,0:T(8,128)S(1)} %fusion.29, bf16[4096,128]{1,0:T(8,128)(2,1)} %all-gather.3.cloned.1.call-done, s32[]{:T(128)S(6)} %select_n.3), kind=kOutput, calls=%fused_computation.2 | convolution fusion | flops 2824077312 | bytes 9306116 | tf_op jit(solution)/shard_map/dot_general | solution.py:38
  46.5 0.0 all-gather.5.cloned.1.call-update
  46.5 0.0 copy-done.1
  46.6 0.1 copy.11
  46.6 0.1 copy.12
  46.7 6.3 %fusion.11 = bf16[48,16,128]{2,1,0:T(8,128)(2,1)S(1)} fusion(bf16[48,16,4096]{2,1,0:T(8,128)(2,1)} %param.7, bf16[4096,128]{1,0:T(8,128)(2,1)} %all-gather.3.cloned.1.call-done, s32[48,8]{1,0:T(8,128)S(1)} %copy.12, s32[48,8]{1,0:T(8,128)S(1)} %copy.11), kind=kOutput, calls=%fused_computation.7 | convolution fusion | flops 843350016 | bytes 7539712 | tf_op jit(solution)/shard_map/mtb,mbc->mtc/dot_general | solution.py:52
  53.1 141.8 %all-gather.5.cloned.1.call-done = bf16[3584,4096]{1,0:T(8,128)(2,1)} async-done(((bf16[3584,512]{1,0:T(8,128)(2,1)}), bf16[3584,4096]{1,0:T(8,128)(2,1)}) %all-gather.5.cloned.1.call-update) | async-done | bytes 29360144 | tf_op jit(solution)/shard_map/all_gather | solution.py:43
  194.8 28.2 %fusion.33 = f32[3584,768]{0,1:T(8,128)S(1)} fusion(bf16[3584,4096]{1,0:T(8,128)(2,1)} %all-gather.5.cloned.1.call-done, bf16[768,4096]{1,0:T(8,128)(2,1)} %bitcast.33), kind=kOutput, calls=%fused_computation.34 | convolution fusion | flops 22548578304 | bytes 46661632 | tf_op jit(solution)/shard_map/dot_general | solution.py:41
  223.0 4.0 %fusion = bf16[768,3584]{1,0:T(8,128)(2,1)} fusion(f32[3584,768]{0,1:T(8,128)S(1)} %fusion.33, bf16[768,128]{1,0:T(8,128)(2,1)S(1)} %bitcast.32, bf16[3584,128]{1,0:T(8,128)(2,1)S(1)} %copy-done), kind=kOutput, calls=%fused_computation.1 | convolution fusion | flops 710148096 | bytes 17629184 | tf_op jit(solution)/shard_map/dot_general | solution.py:53
  (5 shorter events, 0.0 us)
Async XLA Ops:
  7.2 25.0 %copy-start = (bf16[3584,128]{1,0:T(8,128)(2,1)S(1)}, bf16[3584,128]{1,0:T(8,128)(2,1)}, u32[]{:S(2)}) copy-start(bf16[3584,128]{1,0:T(8,128)(2,1)} %param.10) | copy-start | bytes 2752516
  7.2 33.1 %all-gather.3.cloned.1.call-start = ((), (), s32[]{:S(2)}) async-start(), calls=%async_computation | async-start | bytes 1310720 | tf_op jit(solution)/shard_map/all_gather | solution.py:32
  7.9 186.9 %all-gather.5.cloned.1.call-start = ((), (), s32[]{:S(2)}) async-start(), calls=%async_computation.1 | async-start | bytes 33030144 | tf_op jit(solution)/shard_map/all_gather | solution.py:43
  22.2 1.3 collective-permute-start
  23.5 4.3 %collective-permute-start.1 = (f32[128,128]{1,0:T(8,128)S(1)}, f32[128,128]{1,0:T(8,128)S(1)}, u32[]{:S(2)}, u32[]{:S(2)}) collective-permute-start(f32[128,128]{1,0:T(8,128)S(1)} %add.24), channel_id=1, source_target_pairs={{0,8},{4,12},{8,0},{12,4},{16,24},{20,28},{24,16},{28,20},{1,9},{5... | collective-permute-start | bytes 196616 | tf_op jit(solution)/shard_map/ppermute | solution.py:30
  27.9 4.3 %collective-permute-start.2 = (f32[128,128]{1,0:T(8,128)S(1)}, f32[128,128]{1,0:T(8,128)S(1)}, u32[]{:S(2)}, u32[]{:S(2)}) collective-permute-start(f32[128,128]{1,0:T(8,128)S(1)} %add.25), channel_id=1, source_target_pairs={{0,16},{4,20},{8,24},{12,28},{16,0},{20,4},{24,8},{28,12},{1,17},{... | collective-permute-start | bytes 196616 | tf_op jit(solution)/shard_map/ppermute | solution.py:30
  33.1 13.4 %copy-start.1 = (s32[48,2,8]{0,2,1:T(8,128)S(1)}, s32[48,2,8]{0,2,1:T(8,128)}, u32[]{:S(2)}) copy-start(s32[48,2,8]{0,2,1:T(8,128)} %param.13) | copy-start | bytes 9220
Sparse Core Ops, SparseCore 0:
  9.6 30.6 all-gather.2
  46.7 148.1 all-gather.4
